TPU v7x, 32 devices: a whole 2x2x4 slice. The times are simulated.
32 devices in a mesh: south: 4 (over y, x), east: 4 (over z), down: 2 (over core).
Axes of the slice: x: 2, y: 2, z: 4, core: 2. Of those that a mesh axis runs over, the one named last changes fastest.
Arguments:
- field_values: float32 [32, 384, 16, 128], P('south', 'east', 'down'), may hold values from 0.2 to 1.8
- flow_y: float32 [32, 384, 16, 128], P('south', 'east', 'down'), may hold values from -0.3 to 0.3
- flow_x: float32 [32, 384, 16, 128], P('south', 'east', 'down'), may hold values from -0.3 to 0.3
- flow_z: float32 [32, 384, 16, 128], P('south', 'east', 'down'), may hold values from -0.3 to 0.3
Outputs:
- potential: float32 [32, 384, 16, 128], P('south', 'east', 'down')
- field_values_end: float32 [32, 384, 16, 128], P('south', 'east', 'down')
All inputs are finite; a program needn't handle non-finite values.
Results may differ from a plain program's by a relative error of at most 0.00002.
Values sent between devices are 32-bit elements; how exact they have to be, the bound alone decides.
A program may use at most 128 MiB of HBM per device.

v0:
```python
import functools

import jax
import jax.numpy as jnp
from jax import lax
from jax.experimental import pallas as pl
from jax.experimental.pallas import tpu as pltpu
from jax.sharding import PartitionSpec as P

STEPS = 4
AXES = ("south", "east", "down")
MESH = pl.DeviceIdType.MESH


def group_of(columns):
    return next(size for size in (8, 4, 2, 1) if columns % size == 0)


def chunk_of(columns, group):
    return next(size for size in (2 * group, 2 * group, group) if columns % size == 0)


def kernel(sizes, depth, field, flow_y, flow_x, flow_z, pot, end, u, fy, fx, fz,
           faces, halos, totals, totals_in, load_sem, south_recv, east_recv, down_recv,
           tot_recv, south_send, east_send, down_send, tot_send, go):
    rows, cells, levels = field.shape
    columns = cells // depth
    group = group_of(columns)
    width = chunk_of(columns, group)
    chunks = columns // width
    places = {axis: lax.axis_index(axis) for axis in AXES}

    def beside(axis, hop):
        return {axis: lax.rem(places[axis] + hop, sizes[axis])}

    odd = lax.rem(places["south"], 2)
    near = odd
    leads = lax.rem(places["down"], 2) == 0
    follows = jnp.logical_not(leads)
    split = sizes["down"] == 2 and sizes["south"] % 2 == 0 and sizes["south"] > 2
    hops = [(axis, hop) for axis in ("south", "east") for hop in sorted({1, sizes[axis] - 1})]
    barrier = pltpu.get_barrier_semaphore()
    partner = beside("south", 1 + near * (sizes["south"] - 2))

    def greet(device_id):
        pl.semaphore_signal(barrier, inc=1, device_id=device_id, device_id_type=MESH)

    if split:
        @pl.when(leads)
        def _():
            greet(partner)
            greet({"down": 1})

        for axis, hop in hops:
            greet({**beside(axis, hop), "down": 1})
        greeted = jnp.where(leads, 1, 2 * len(hops) + 1)
    else:
        hops += [("down", hop) for hop in range(1, sizes["down"])]
        for axis, hop in hops:
            greet(beside(axis, hop))
        greeted = len(hops)

    def load(src, dst, sem):
        return pltpu.make_async_copy(src, dst, load_sem.at[sem])

    def done(ref, sem):
        pltpu.make_async_copy(ref, ref, sem).wait()

    def rows_of(t, start, count):
        return u.at[t, pl.ds(start, count), pl.ds(depth, cells), :]

    rims = [load(field.at[pl.ds(y, 1)], rows_of(0, y + 1, 1), 0) for y in (0, rows - 1)]
    inner = load(field.at[pl.ds(1, rows - 2)], rows_of(0, 2, rows - 2), 1)
    flows = [load(src, dst, 2) for src, dst in ((flow_y, fy), (flow_x, fx), (flow_z, fz))]
    for copy in rims:
        copy.start()
    done(rows_of(0, 1, 2), load_sem.at[0])
    inner.start()
    for copy in flows:
        copy.start()
    pl.semaphore_wait(barrier, greeted)

    def south(t, side, c):
        at = pl.multiple_of(c * width * depth, 8)
        return pltpu.make_async_remote_copy(
            src_ref=u.at[t, (1 - side) * (rows - 1) + 1, pl.ds(at + depth, width * depth), :],
            dst_ref=u.at[t, side * (rows + 1), pl.ds(at + depth, width * depth), :],
            send_sem=south_send, recv_sem=south_recv.at[t % 2, c],
            device_id=beside("south", 1 + side * (sizes["south"] - 2)), device_id_type=MESH)

    def south_done(t, c):
        at = pl.multiple_of(c * width * depth, 8)
        done(u.at[t, pl.ds(0, 2), pl.ds(at + depth, width * depth), :], south_recv.at[t % 2, c])

    blocks = ((1, rows - 2), (0, 1), (rows - 1, 1))

    def east(t, side, part):
        start, count = blocks[part]
        column = columns if side == 0 else 1
        if t == 0:
            src = field.at[pl.ds(start, count), pl.ds((column - 1) * depth, depth), :]
        else:
            src = u.at[t, pl.ds(start + 1, count), pl.ds(column * depth, depth), :]
        return pltpu.make_async_remote_copy(
            src_ref=src,
            dst_ref=u.at[t, pl.ds(start + 1, count), pl.ds(0 if side == 0 else cells + depth, depth), :],
            send_sem=east_send, recv_sem=east_recv.at[t % 2, min(part, 1)],
            device_id=beside("east", 1 if side == 0 else sizes["east"] - 1), device_id_type=MESH)

    def down(t, side, part):
        start, count = blocks[part]
        return pltpu.make_async_remote_copy(
            src_ref=faces.at[t, side, pl.ds(start, count)],
            dst_ref=halos.at[t, side, pl.ds(start, count)],
            send_sem=down_send, recv_sem=down_recv.at[t % 2, min(part, 1)],
            device_id=beside("down", 1 if side == 0 else sizes["down"] - 1), device_id_type=MESH)

    def sides_start(t, parts):
        for part in parts:
            for side in (0, 1):
                down(t, side, part).start()
                east(t, side, part).start()

    def sides_done(t, part):
        count = rows - 2 if part == 0 else 2
        done(u.at[t, pl.ds(0, count), pl.ds(0, 2 * depth), :], east_recv.at[t % 2, part])
        done(halos.at[t, :, pl.ds(0, count)], down_recv.at[t % 2, part])

    def total(hop, piece, y0, count, x0, span):
        cut = (pl.ds(y0, count), pl.ds(x0, span))
        return pltpu.make_async_remote_copy(
            src_ref=totals.at[cut], dst_ref=totals_in.at[(hop - 1, *cut)],
            send_sem=tot_send.at[hop - 1], recv_sem=tot_recv.at[hop - 1, piece],
            device_id=beside("down", hop), device_id_type=MESH)

    def rim_at(c):
        return pl.multiple_of(c * width, group)

    place_in_block = lax.broadcasted_iota(jnp.int32, (depth, levels), 0)
    on_first, on_last = place_in_block == 0, place_in_block == depth - 1

    def take_faces(t, y, x0):
        for side, place in ((0, depth - 1), (1, 0)):
            start = (x0 + 1) * depth + place
            faces[t, side, y, pl.ds(x0, group), :] = u[t, y + 1, pl.ds(start, group, stride=depth), :]

    def march(t, y, x0):
        def at(x, pad):
            return pl.ds(pl.multiple_of((x + pad) * depth, 8), depth)

        line = [u[t - 1, y + 1, at(x0 + g, 0), :] for g in range(group + 2)]
        for g in range(group):
            x = x0 + g
            mid, west, east_of = line[g + 1], line[g], line[g + 2]
            north, south_of = u[t - 1, y, at(x, 1), :], u[t - 1, y + 2, at(x, 1), :]
            low = jnp.broadcast_to(halos[t - 1, 0, y, pl.ds(x, 1), :], (depth, levels))
            high = jnp.broadcast_to(halos[t - 1, 1, y, pl.ds(x, 1), :], (depth, levels))
            low = jnp.where(on_first, low, pltpu.roll(mid, 1, 0))
            high = jnp.where(on_last, high, pltpu.roll(mid, depth - 1, 0))
            own = at(x, 0)
            spread = (north + south_of) + (west + east_of) + (low + high) - 6.0 * mid
            value = (mid - fy[y, own, :] * (south_of - north) - fx[y, own, :] * (east_of - west)
                     - fz[y, own, :] * (high - low) + 0.05 * spread)
            if t < STEPS:
                u[t, y + 1, at(x, 1), :] = value
            else:
                end[y, own, :] = value
                hop = 1
                while hop < depth:
                    value = value + jnp.where(place_in_block >= hop, pltpu.roll(value, hop, 0), 0.0)
                    hop *= 2
                pot[y, own, :] = value
        if t < STEPS:
            take_faces(t, y, x0)
        else:
            start = x0 * depth + depth - 1
            totals[y, pl.ds(x0, group), :] = pot[y, pl.ds(start, group, stride=depth), :]

    def over(y0, count, x0, span, body):
        groups = span // group

        def one(i, carry):
            body(y0 + i // groups, pl.multiple_of(x0 + (i % groups) * group, group))
            return carry

        lax.fori_loop(0, count * groups, one, 0)

    def finish(y, x0):
        for g in range(group):
            own = pl.ds(pl.multiple_of((x0 + g) * depth, 8), depth)
            value = pot[y, own, :]
            for hop in range(1, sizes["down"]):
                below = jnp.broadcast_to(totals_in[hop - 1, y, pl.ds(x0 + g, 1), :], (depth, levels))
                value = value + jnp.where(places["down"] >= hop, below, 0.0)
            pot[y, own, :] = value * (1.0 / (depth * sizes["down"]))

    down_hops = range(1, sizes["down"])

    def each(count, body):
        def one(i, carry):
            body(i)
            return carry

        lax.fori_loop(0, count, one, 0)

    def upwards(body):
        for hop in down_hops:
            pl.when(places["down"] + hop < sizes["down"])(functools.partial(body, hop))

    def from_below(body):
        for hop in down_hops:
            pl.when(places["down"] >= hop)(functools.partial(body, hop))

    def rim_over(c, body):
        groups = width // group

        def one(i):
            body((i // groups) * (rows - 1), pl.multiple_of(c * width + (i % groups) * group, group))

        each(2 * groups, one)

    def send_chunk(t, c):
        south(t, 1 - near, c).start()
        south(t, near, c).start()

    def send_first():
        each(chunks, lambda c: send_chunk(0, c))

    def send_rim_totals(c):
        def one(hop):
            for y in (0, rows - 1):
                total(hop, 1 + c, y, 1, rim_at(c), width).start()

        upwards(one)

    def finish_rim(c):
        from_below(lambda hop: done(totals_in.at[hop - 1, pl.ds(0, 2), pl.ds(rim_at(c), width)],
                                    tot_recv.at[hop - 1, 1 + c]))
        rim_over(c, finish)

    if split:
        @pl.when(leads)
        def _():
            each(chunks, lambda c: south(0, near, c).start())

        @pl.when(follows)
        def _():
            pl.semaphore_signal(go, inc=1, device_id={"down": 0}, device_id_type=MESH)
    else:
        pl.when(leads)(send_first)
    done(rows_of(0, 2, rows - 2), load_sem.at[1])
    over(0, rows, 0, columns, functools.partial(take_faces, 0))
    if split:
        @pl.when(leads)
        def _():
            pl.semaphore_wait(go, 1)
            each(chunks, lambda c: south(0, 1 - near, c).start())
    sides_start(0, (0, 1, 2))
    pl.when(follows)(send_first)
    done(u.at[pl.ds(0, 3), pl.ds(0, rows), pl.ds(depth, cells), :], load_sem.at[2])

    for t in range(1, STEPS + 1):
        sides_done(t - 1, 0)
        over(*blocks[0], 0, columns, functools.partial(march, t))
        if t < STEPS:
            sides_start(t, (0,))
        else:
            upwards(lambda hop: total(hop, 0, *blocks[0], 0, columns).start())
            from_below(lambda hop: total(hop, 0, *blocks[0], 0, columns).wait_recv())
            over(*blocks[0], 0, columns, finish)
        sides_done(t - 1, 1)

        def rim(c):
            south_done(t - 1, c)
            rim_over(c, functools.partial(march, t))
            if t < STEPS:
                send_chunk(t, c)
            else:
                send_rim_totals(c)
                pl.when(c > 0)(lambda: finish_rim(c - 1))

        each(chunks, rim)
        if t < STEPS:
            sides_start(t, (1, 2))
    finish_rim(chunks - 1)
    done(u.at[:, pl.ds(0, 2), pl.ds(depth, cells), :], south_send)
    done(u.at[:, pl.ds(0, rows), pl.ds(0, 2 * depth), :], east_send)
    done(faces, down_send)
    upwards(lambda hop: done(totals, tot_send.at[hop - 1]))


def write_out(*refs):
    count = len(refs) // 2
    sems = refs[-1]
    pairs = list(zip(refs[:count], refs[count:-1]))
    for i, (src, dst) in enumerate(pairs):
        for row in range(src.shape[0]):
            pltpu.make_async_copy(src.at[row], dst.at[row], sems.at[i]).start()
    for i, (src, dst) in enumerate(pairs):
        pltpu.make_async_copy(src, dst, sems.at[i]).wait()


def local(sizes, field_values, *flows):
    rows, columns, depth, levels = field_values.shape
    cells = columns * depth
    width = chunk_of(columns, group_of(columns))
    flat = [array.reshape(rows, cells, levels) for array in (field_values, *flows)]
    block = pltpu.VMEM((rows, cells, levels), jnp.float32)
    dma = pltpu.SemaphoreType.DMA
    others = sizes["down"] - 1
    face = (rows, columns, levels)
    out = jax.ShapeDtypeStruct((rows, cells, levels), jnp.float32)
    held = pl.pallas_call(
        functools.partial(kernel, sizes, depth),
        out_shape=(block, block),
        in_specs=[pl.BlockSpec(memory_space=pl.ANY)] * 4,
        out_specs=(pl.BlockSpec(memory_space=pltpu.VMEM),) * 2,
        scratch_shapes=[
            pltpu.VMEM((STEPS, rows + 2, cells + 2 * depth, levels), jnp.float32),
            block, block, block,
            pltpu.VMEM((STEPS, 2, *face), jnp.float32),
            pltpu.VMEM((STEPS, 2, *face), jnp.float32),
            pltpu.VMEM(face, jnp.float32),
            pltpu.VMEM((others, *face), jnp.float32),
            dma((3,)),
            dma((2, columns // width)), dma((2, 2)), dma((2, 2)), dma((others, 1 + columns // width)),
            dma, dma, dma, dma((others,)),
            pltpu.SemaphoreType.REGULAR,
        ],
        compiler_params=pltpu.CompilerParams(
            collective_id=0, has_side_effects=True, vmem_limit_bytes=48 * 1024 * 1024),
    )(*flat)
    results = pl.pallas_call(
        write_out,
        out_shape=(out, out),
        in_specs=[pl.BlockSpec(memory_space=pltpu.VMEM)] * 2,
        out_specs=(pl.BlockSpec(memory_space=pltpu.HBM),) * 2,
        scratch_shapes=[dma((2,))],
        compiler_params=pltpu.CompilerParams(vmem_limit_bytes=8 * 1024 * 1024),
    )(*held)
    return tuple(array.reshape(rows, columns, depth, levels) for array in results)


def solution(mesh):
    spec = P("south", "east", "down", None)
    sizes = {axis: mesh.shape[axis] for axis in AXES}
    return jax.shard_map(
        functools.partial(local, sizes), mesh=mesh, in_specs=(spec,) * 4,
        out_specs=(spec, spec), check_vma=False)
```

profile of v0, /device:TPU:5, one launch (start us, length us, event | category | flops | bytes accessed | tf_op | source)
XLA Modules:
  0.0 75.6 jit_solution(16489741599245592427)
XLA Ops:
  0.6 72.3 %shard_map.59 = (f32[8,768,128]{2,1,0:T(8,128)S(1)}, f32[8,768,128]{2,1,0:T(8,128)S(1)}) custom-call(f32[8,768,128]{2,1,0:T(8,128)} %bitcast.6, f32[8,768,128]{2,1,0:T(8,128)} %bitcast.7, f32[8,768,128]{2,1,0:T(8,128)} %bitcast.8, f32[8,768,128]{2,1,0:T(8,128)} %bitcast.9), custom_call_target="tpu_custom_call" | custom-call | tf_op jit(solution)/shard_map/pallas_call | solution.py:313
  72.9 2.7 %shard_map.60 = (f32[8,768,128]{2,1,0:T(8,128)}, f32[8,768,128]{2,1,0:T(8,128)}) custom-call(f32[8,768,128]{2,1,0:T(8,128)S(1)} %get-tuple-element.6.refs_0_, f32[8,768,128]{2,1,0:T(8,128)S(1)} %get-tuple-element.7.refs_1_), custom_call_target="tpu_custom_call" | custom-call | tf_op jit(solution)/shard_map/pallas_call | solution.py:333
where the time goes:
time: 76.8 us; the launch traced here: 75.6 us
  Pallas kernels  75 us (98%)
    pallas_call x1, Pallas kernels, local(): pl.pallas_call(functools.partial(kernel, sizes, depth), out_shape=(block,...  72.3 us
    pallas_call x1, Pallas kernels, local(): pl.pallas_call(write_out, out_shape=(out, out), in_specs=[pl.BlockSpec(me...  2.66 us

commit v1 on v0

--- a/solution.py
+++ b/solution.py
@@ -46,14 +46,14 @@
         pl.semaphore_signal(barrier, inc=1, device_id=device_id, device_id_type=MESH)
 
     if split:
-        @pl.when(leads)
+        @pl.when(follows)
         def _():
             greet(partner)
-            greet({"down": 1})
+            greet({"down": 0})
 
         for axis, hop in hops:
-            greet({**beside(axis, hop), "down": 1})
-        greeted = jnp.where(leads, 1, 2 * len(hops) + 1)
+            greet({**beside(axis, hop), "down": 0})
+        greeted = jnp.where(follows, 1, 2 * len(hops) + 1)
     else:
         hops += [("down", hop) for hop in range(1, sizes["down"])]
         for axis, hop in hops:
@@ -69,12 +69,21 @@
     def rows_of(t, start, count):
         return u.at[t, pl.ds(start, count), pl.ds(depth, cells), :]
 
-    rims = [load(field.at[pl.ds(y, 1)], rows_of(0, y + 1, 1), 0) for y in (0, rows - 1)]
-    inner = load(field.at[pl.ds(1, rows - 2)], rows_of(0, 2, rows - 2), 1)
-    flows = [load(src, dst, 2) for src, dst in ((flow_y, fy), (flow_x, fx), (flow_z, fz))]
-    for copy in rims:
+    def rim_piece(side, start, count, sem):
+        y = (1 - side) * (rows - 1)
+        return load(field.at[y, pl.ds(start, count)], u.at[0, y + 1, pl.ds(depth + start, count), :], sem)
+
+    early = min(1, chunks)
+    head = early * width * depth
+    rest = [rim_piece(1 - near, 0, cells, 1)]
+    if head < cells:
+        rest.append(rim_piece(near, head, cells - head, 1))
+    inner = load(field.at[pl.ds(1, rows - 2)], rows_of(0, 2, rows - 2), 2)
+    flows = [load(src, dst, 3) for src, dst in ((flow_y, fy), (flow_x, fx), (flow_z, fz))]
+    rim_piece(near, 0, head, 0).start()
+    for copy in rest:
         copy.start()
-    done(rows_of(0, 1, 2), load_sem.at[0])
+    done(u.at[0, 0, pl.ds(0, head), :], load_sem.at[0])
     inner.start()
     for copy in flows:
         copy.start()
@@ -91,6 +100,9 @@
     def south_done(t, c):
         at = pl.multiple_of(c * width * depth, 8)
         done(u.at[t, pl.ds(0, 2), pl.ds(at + depth, width * depth), :], south_recv.at[t % 2, c])
+
+    def rest_done():
+        done(u.at[pl.ds(0, 2), 0, pl.ds(0, cells - head // 2), :], load_sem.at[1])
 
     blocks = ((1, rows - 2), (0, 1), (rows - 1, 1))
 
@@ -223,6 +235,14 @@
         south(t, 1 - near, c).start()
         south(t, near, c).start()
 
+    last_block = sizes["south"] - 1
+    first = jnp.where(places["south"] == last_block, 0, jnp.where(places["south"] == 1, 1, 1 - near))
+    lag = min(4, chunks)
+
+    def send_last(c):
+        south(STEPS - 1, first, c).start()
+        pl.when(c >= lag)(lambda: south(STEPS - 1, 1 - first, c - lag).start())
+
     def send_first():
         each(chunks, lambda c: send_chunk(0, c))
 
@@ -238,30 +258,57 @@
                                     tot_recv.at[hop - 1, 1 + c]))
         rim_over(c, finish)
 
+    def send_far():
+        each(chunks, lambda c: south(0, 1 - near, c).start())
+
+    if split:
+        @pl.when(follows)
+        def _():
+            each(early, lambda c: south(0, near, c).start())
+
+        @pl.when(leads)
+        def _():
+            pl.semaphore_signal(go, inc=1, device_id={"down": 1}, device_id_type=MESH)
+
+        rest_done()
+
+        @pl.when(follows)
+        def _():
+            each(chunks - early, lambda c: south(0, near, early + c).start())
+    else:
+        rest_done()
+    pl.when(leads)(send_first)
+    done(rows_of(0, 2, rows - 2), load_sem.at[2])
+    over(0, rows, 0, columns, functools.partial(take_faces, 0))
+    if split:
+        pl.when(follows)(lambda: pl.semaphore_wait(go, 1))
+    sides_start(0, (0, 1, 2))
+    if not split:
+        pl.when(follows)(send_first)
+    done(u.at[pl.ds(0, 3), pl.ds(0, rows), pl.ds(depth, cells), :], load_sem.at[3])
+
+    ahead = min(3, chunks) if split else 0
     if split:
         @pl.when(leads)
         def _():
-            each(chunks, lambda c: south(0, near, c).start())
-
-        @pl.when(follows)
-        def _():
-            pl.semaphore_signal(go, inc=1, device_id={"down": 0}, device_id_type=MESH)
-    else:
-        pl.when(leads)(send_first)
-    done(rows_of(0, 2, rows - 2), load_sem.at[1])
-    over(0, rows, 0, columns, functools.partial(take_faces, 0))
-    if split:
-        @pl.when(leads)
-        def _():
-            pl.semaphore_wait(go, 1)
-            each(chunks, lambda c: south(0, 1 - near, c).start())
-    sides_start(0, (0, 1, 2))
-    pl.when(follows)(send_first)
-    done(u.at[pl.ds(0, 3), pl.ds(0, rows), pl.ds(depth, cells), :], load_sem.at[2])
+            each(ahead, lambda c: south_done(0, c))
+            pl.semaphore_signal(go, inc=1, device_id={"down": 1}, device_id_type=MESH)
+
+    def take_south(t, c):
+        if t == 0 and split:
+            pl.when(jnp.logical_or(follows, c >= ahead))(lambda: south_done(t, c))
+        else:
+            south_done(t, c)
 
     for t in range(1, STEPS + 1):
         sides_done(t - 1, 0)
         over(*blocks[0], 0, columns, functools.partial(march, t))
+        if t == 1 and split:
+            @pl.when(follows)
+            def _():
+                pl.semaphore_wait(go, 1)
+                send_far()
+
         if t < STEPS:
             sides_start(t, (0,))
         else:
@@ -271,15 +318,19 @@
         sides_done(t - 1, 1)
 
         def rim(c):
-            south_done(t - 1, c)
+            take_south(t - 1, c)
             rim_over(c, functools.partial(march, t))
-            if t < STEPS:
+            if t < STEPS - 1:
                 send_chunk(t, c)
+            elif t < STEPS:
+                send_last(c)
             else:
                 send_rim_totals(c)
                 pl.when(c > 0)(lambda: finish_rim(c - 1))
 
         each(chunks, rim)
+        if t == STEPS - 1:
+            each(lag, lambda c: south(t, 1 - first, chunks - lag + c).start())
         if t < STEPS:
             sides_start(t, (1, 2))
     finish_rim(chunks - 1)
@@ -322,7 +373,7 @@
             pltpu.VMEM((STEPS, 2, *face), jnp.float32),
             pltpu.VMEM(face, jnp.float32),
             pltpu.VMEM((others, *face), jnp.float32),
-            dma((3,)),
+            dma((4,)),
             dma((2, columns // width)), dma((2, 2)), dma((2, 2)), dma((others, 1 + columns // width)),
             dma, dma, dma, dma((others,)),
             pltpu.SemaphoreType.REGULAR,

time: 76.8 us -> 74.6 us (0.971); the launches traced: 75.6 us -> 74.5 us
  Pallas kernels: 75 us -> 73.8 us
    pallas_call x1, Pallas kernels: 72.3 us -> 71.2 us  [local(): pl.pallas_call(functools.partial(kernel, sizes, depth), out_shape=(block,...]
where the time goes in v1:
time: 74.6 us; the launch traced here: 74.5 us
  Pallas kernels  73.8 us (99%)
    pallas_call x1, Pallas kernels, local(): pl.pallas_call(functools.partial(kernel, sizes, depth), out_shape=(block,...  71.2 us
    pallas_call x1, Pallas kernels, local(): pl.pallas_call(write_out, out_shape=(out, out), in_specs=[pl.BlockSpec(me...  2.66 us

profile of v1, /device:TPU:5, one launch (start us, length us, event | category | flops | bytes accessed | tf_op | source)
XLA Modules:
  0.0 74.5 jit_solution(14766277250894927459)
XLA Ops:
  0.6 71.2 %shard_map.59 = (f32[8,768,128]{2,1,0:T(8,128)S(1)}, f32[8,768,128]{2,1,0:T(8,128)S(1)}) custom-call(f32[8,768,128]{2,1,0:T(8,128)} %bitcast.6, f32[8,768,128]{2,1,0:T(8,128)} %bitcast.7, f32[8,768,128]{2,1,0:T(8,128)} %bitcast.8, f32[8,768,128]{2,1,0:T(8,128)} %bitcast.9), custom_call_target="tpu_custom_call" | custom-call | tf_op jit(solution)/shard_map/pallas_call | solution.py:364
  71.8 2.7 %shard_map.60 = (f32[8,768,128]{2,1,0:T(8,128)}, f32[8,768,128]{2,1,0:T(8,128)}) custom-call(f32[8,768,128]{2,1,0:T(8,128)S(1)} %get-tuple-element.6.refs_0_, f32[8,768,128]{2,1,0:T(8,128)S(1)} %get-tuple-element.7.refs_1_), custom_call_target="tpu_custom_call" | custom-call | tf_op jit(solution)/shard_map/pallas_call | solution.py:384

commit v2 on v1

v2 whole, which is shorter than its diff:
```python
import functools

import jax
import jax.numpy as jnp
from jax import lax
from jax.experimental import pallas as pl
from jax.experimental.pallas import tpu as pltpu
from jax.sharding import PartitionSpec as P

STEPS = 4
AXES = ("south", "east", "down")
MESH = pl.DeviceIdType.MESH


def group_of(columns):
    return next(size for size in (8, 4, 2, 1) if columns % size == 0)


def chunk_of(columns, group):
    return next(size for size in (2 * group, group) if columns % size == 0)


def each(count, body):
    def one(i, carry):
        body(i)
        return carry

    lax.fori_loop(0, count, one, 0)


def new_values(depth, group, u, halos, fy, fx, fz, t, y, row, x0):
    levels = u.shape[-1]
    place = lax.broadcasted_iota(jnp.int32, (depth, levels), 0)

    def at(x, pad):
        return pl.ds(pl.multiple_of((x + pad) * depth, 8), depth)

    line = [u[t - 1, y + 1, at(x0 + g, 0), :] for g in range(group + 2)]
    values = []
    for g in range(group):
        x = x0 + g
        mid, west, east_of = line[g + 1], line[g], line[g + 2]
        north, south_of = u[t - 1, y, at(x, 1), :], u[t - 1, y + 2, at(x, 1), :]
        low = jnp.broadcast_to(halos[t - 1, 0, row, pl.ds(x, 1), :], (depth, levels))
        high = jnp.broadcast_to(halos[t - 1, 1, row, pl.ds(x, 1), :], (depth, levels))
        low = jnp.where(place == 0, low, pltpu.roll(mid, 1, 0))
        high = jnp.where(place == depth - 1, high, pltpu.roll(mid, depth - 1, 0))
        own = at(x, 0)
        spread = (north + south_of) + (west + east_of) + (low + high) - 6.0 * mid
        values.append(mid - fy[row, own, :] * (south_of - north) - fx[row, own, :] * (east_of - west)
                      - fz[row, own, :] * (high - low) + 0.05 * spread)
    return values


def running_sum(value):
    depth = value.shape[0]
    place = lax.broadcasted_iota(jnp.int32, value.shape, 0)
    hop = 1
    while hop < depth:
        value = value + jnp.where(place >= hop, pltpu.roll(value, hop, 0), 0.0)
        hop *= 2
    return value


def finished(sizes, totals_in, row, x, value):
    rank = lax.axis_index("down")
    for hop in range(1, sizes["down"]):
        below = jnp.broadcast_to(totals_in[hop - 1, row, pl.ds(x, 1), :], value.shape)
        value = value + jnp.where(rank >= hop, below, 0.0)
    return value * (1.0 / (value.shape[0] * sizes["down"]))


def kernel(sizes, depth, field, flow_y, flow_x, flow_z, pot, end, last_u, last_flows, last_halos, last_totals,
           u, fy, fx, fz, faces, halos, totals, totals_in, load_sem, south_recv, side_recv, tot_recv, south_send, side_send, tot_send, go):
    rows, cells, levels = field.shape
    columns = cells // depth
    group = group_of(columns)
    width = chunk_of(columns, group)
    chunks = columns // width
    places = {axis: lax.axis_index(axis) for axis in AXES}

    def beside(axis, hop):
        return {axis: lax.rem(places[axis] + hop, sizes[axis])}

    near = lax.rem(places["south"], 2)
    leads = lax.rem(places["down"], 2) == 0
    follows = jnp.logical_not(leads)
    split = sizes["down"] == 2 and sizes["south"] % 2 == 0 and sizes["south"] > 2
    hops = [(axis, hop) for axis in ("south", "east") for hop in sorted({1, sizes[axis] - 1})]
    barrier = pltpu.get_barrier_semaphore()
    partner = beside("south", 1 + near * (sizes["south"] - 2))

    def greet(device_id):
        pl.semaphore_signal(barrier, inc=1, device_id=device_id, device_id_type=MESH)

    if split:
        @pl.when(follows)
        def _():
            greet(partner)
            greet({"down": 0})

        for axis, hop in hops:
            greet({**beside(axis, hop), "down": 0})
        greeted = jnp.where(follows, 1, 2 * len(hops) + 1)
    else:
        hops += [("down", hop) for hop in range(1, sizes["down"])]
        for axis, hop in hops:
            greet(beside(axis, hop))
        greeted = len(hops)

    def load(src, dst, sem):
        return pltpu.make_async_copy(src, dst, load_sem.at[sem])

    def done(ref, sem):
        pltpu.make_async_copy(ref, ref, sem).wait()

    def rim_piece(side, start, count, sem):
        y = (1 - side) * (rows - 1)
        return load(field.at[y, pl.ds(start, count)], u.at[0, y + 1, pl.ds(depth + start, count), :], sem)

    early = min(1, chunks)
    head = early * width * depth
    rest = [rim_piece(1 - near, 0, cells, 1)]
    if head < cells:
        rest.append(rim_piece(near, head, cells - head, 1))
    inner = load(field.at[pl.ds(1, rows - 2)], u.at[0, pl.ds(2, rows - 2), pl.ds(depth, cells), :], 2)
    flows = [load(src, dst, 3) for src, dst in ((flow_y, fy), (flow_x, fx), (flow_z, fz))]
    rim_piece(near, 0, head, 0).start()
    for copy in rest:
        copy.start()
    done(u.at[0, 0, pl.ds(0, head), :], load_sem.at[0])
    inner.start()
    for copy in flows:
        copy.start()
    pl.semaphore_wait(barrier, greeted)

    def rest_done():
        done(u.at[pl.ds(0, 2), 0, pl.ds(0, cells - head // 2), :], load_sem.at[1])

    def chunk_at(c):
        return pl.ds(pl.multiple_of(c * width * depth + depth, 8), width * depth)

    def south(t, side, c):
        return pltpu.make_async_remote_copy(
            src_ref=u.at[t, (1 - side) * (rows - 1) + 1, chunk_at(c), :],
            dst_ref=u.at[t, side * (rows + 1), chunk_at(c), :],
            send_sem=south_send, recv_sem=south_recv.at[t % 2, c],
            device_id=beside("south", 1 + side * (sizes["south"] - 2)), device_id_type=MESH)

    def south_done(t, c):
        done(u.at[t, pl.ds(0, 2), chunk_at(c), :], south_recv.at[t % 2, c])

    blocks = ((1, rows - 2), (0, 1), (rows - 1, 1))

    def east(t, side, part):
        start, count = blocks[part]
        column = columns if side == 0 else 1
        if t == 0:
            src = field.at[pl.ds(start, count), pl.ds((column - 1) * depth, depth), :]
        else:
            src = u.at[t, pl.ds(start + 1, count), pl.ds(column * depth, depth), :]
        return pltpu.make_async_remote_copy(
            src_ref=src,
            dst_ref=u.at[t, pl.ds(start + 1, count), pl.ds(0 if side == 0 else cells + depth, depth), :],
            send_sem=side_send, recv_sem=side_recv.at[t % 2, min(part, 1)],
            device_id=beside("east", 1 if side == 0 else sizes["east"] - 1), device_id_type=MESH)

    def down(t, side, part):
        start, count = blocks[part]
        return pltpu.make_async_remote_copy(
            src_ref=faces.at[t, side, pl.ds(start, count)],
            dst_ref=halos.at[t, side, pl.ds(start, count)],
            send_sem=side_send, recv_sem=side_recv.at[t % 2, min(part, 1)],
            device_id=beside("down", 1 if side == 0 else sizes["down"] - 1), device_id_type=MESH)

    def sides_start(t, parts):
        for part in parts:
            for side in (0, 1):
                down(t, side, part).start()
                east(t, side, part).start()

    both = 2 * (depth + columns)

    def sides_done(t, part):
        done(u.at[t, pl.ds(0, rows - 2 if part == 0 else 2), pl.ds(0, both), :], side_recv.at[t % 2, part])

    def total(hop, piece, y0, count, x0, span):
        cut = (pl.ds(y0, count), pl.ds(x0, span))
        return pltpu.make_async_remote_copy(
            src_ref=totals.at[cut], dst_ref=totals_in.at[(hop - 1, *cut)],
            send_sem=tot_send.at[hop - 1], recv_sem=tot_recv.at[hop - 1, piece],
            device_id=beside("down", hop), device_id_type=MESH)

    def rim_at(c):
        return pl.multiple_of(c * width, group)

    def take_faces(t, y, x0):
        for side, place in ((0, depth - 1), (1, 0)):
            start = (x0 + 1) * depth + place
            faces[t, side, y, pl.ds(x0, group), :] = u[t, y + 1, pl.ds(start, group, stride=depth), :]

    def march(t, y, x0):
        values = new_values(depth, group, u, halos, fy, fx, fz, t, y, y, x0)
        for g, value in enumerate(values):
            if t < STEPS:
                u[t, y + 1, pl.ds(pl.multiple_of((x0 + g + 1) * depth, 8), depth), :] = value
            else:
                own = pl.ds(pl.multiple_of((x0 + g) * depth, 8), depth)
                end[y, own, :] = value
                pot[y, own, :] = running_sum(value)
        if t < STEPS:
            take_faces(t, y, x0)
        else:
            start = x0 * depth + depth - 1
            totals[y, pl.ds(x0, group), :] = pot[y, pl.ds(start, group, stride=depth), :]

    def over(y0, count, x0, span, body):
        groups = span // group
        each(count * groups,
             lambda i: body(y0 + i // groups, pl.multiple_of(x0 + (i % groups) * group, group)))

    def finish(y, x0):
        for g in range(group):
            own = pl.ds(pl.multiple_of((x0 + g) * depth, 8), depth)
            pot[y, own, :] = finished(sizes, totals_in, y, x0 + g, pot[y, own, :])

    down_hops = range(1, sizes["down"])
    last_rank = sizes["down"] - 1

    def upwards(body):
        for hop in down_hops:
            pl.when(places["down"] + hop <= last_rank)(functools.partial(body, hop))

    def from_below(body):
        for hop in down_hops:
            pl.when(places["down"] >= hop)(functools.partial(body, hop))

    def rim_over(c, body):
        groups = width // group
        each(2 * groups, lambda i: body((i // groups) * (rows - 1),
                                        pl.multiple_of(c * width + (i % groups) * group, group)))

    last_block = sizes["south"] - 1
    first = jnp.where(places["south"] == last_block, 0, jnp.where(places["south"] == 1, 1, 1 - near))
    lag = min(4, chunks)

    def send_chunk(t, c):
        south(t, 1 - near, c).start()
        south(t, near, c).start()

    def send_last(c):
        south(STEPS - 1, first, c).start()
        pl.when(c >= lag)(lambda: south(STEPS - 1, 1 - first, c - lag).start())

    def send_first():
        each(chunks, lambda c: send_chunk(0, c))

    def send_far():
        each(chunks, lambda c: south(0, 1 - near, c).start())

    def send_rim_totals(c):
        def one(hop):
            for y in (0, rows - 1):
                total(hop, 1 + c, y, 1, rim_at(c), width).start()

        upwards(one)

    def take_rim_totals(c):
        from_below(lambda hop: done(totals_in.at[hop - 1, pl.ds(0, 2), pl.ds(rim_at(c), width)],
                                    tot_recv.at[hop - 1, 1 + c]))

    def finish_rim(c):
        take_rim_totals(c)
        rim_over(c, finish)

    base = columns - width
    last_cells = pl.ds(base * depth, width * depth)

    def keep_last():
        for side in (0, 1):
            row = side * (rows - 1)
            for i in (0, 1, 2):
                if (side, i) not in ((0, 0), (1, 2)):
                    last_u[0, 3 * side + i] = u[STEPS - 1, row + i, pl.ds(base * depth, (width + 2) * depth), :]
            for i, flow in enumerate((fy, fx, fz)):
                last_flows[i, side] = flow[row, last_cells, :]
            for z in (0, 1):
                last_halos[0, z, side] = halos[STEPS - 1, z, row, pl.ds(base, width), :]

    def keep_south():
        for side in (0, 1):
            last_u[0, 5 * side, pl.ds(depth, width * depth), :] = u[
                STEPS - 1, side * (rows + 1), pl.ds((base + 1) * depth, width * depth), :]

    def keep_totals():
        for hop in down_hops:
            for side in (0, 1):
                @pl.when(places["down"] >= hop)
                def _():
                    last_totals[hop - 1, side] = totals_in[hop - 1, side * (rows - 1), pl.ds(base, width), :]

                @pl.when(places["down"] < hop)
                def _():
                    last_totals[hop - 1, side] = jnp.zeros((width, levels), jnp.float32)

    if split:
        @pl.when(follows)
        def _():
            each(early, lambda c: south(0, near, c).start())

        @pl.when(leads)
        def _():
            pl.semaphore_signal(go, inc=1, device_id={"down": 1}, device_id_type=MESH)

        rest_done()

        @pl.when(follows)
        def _():
            each(chunks - early, lambda c: south(0, near, early + c).start())
    else:
        rest_done()
    pl.when(leads)(send_first)
    done(u.at[0, pl.ds(2, rows - 2), pl.ds(depth, cells), :], load_sem.at[2])
    over(0, rows, 0, columns, functools.partial(take_faces, 0))
    if split:
        pl.when(follows)(lambda: pl.semaphore_wait(go, 1))
    sides_start(0, (0, 1, 2))
    if not split:
        pl.when(follows)(send_first)
    done(u.at[pl.ds(0, 3), pl.ds(0, rows), pl.ds(depth, cells), :], load_sem.at[3])

    ahead = min(3, chunks) if split else 0
    if split:
        @pl.when(leads)
        def _():
            each(ahead, lambda c: south_done(0, c))
            pl.semaphore_signal(go, inc=1, device_id={"down": 1}, device_id_type=MESH)

    def take_south(t, c):
        if t == 0 and split:
            pl.when(jnp.logical_or(follows, c >= ahead))(lambda: south_done(t, c))
        else:
            south_done(t, c)

    for t in range(1, STEPS + 1):
        sides_done(t - 1, 0)
        over(*blocks[0], 0, columns, functools.partial(march, t))
        if t == 1 and split:
            @pl.when(follows)
            def _():
                pl.semaphore_wait(go, 1)
                send_far()

        if t < STEPS:
            sides_start(t, (0,))
        else:
            upwards(lambda hop: total(hop, 0, *blocks[0], 0, columns).start())
            from_below(lambda hop: total(hop, 0, *blocks[0], 0, columns).wait_recv())
            over(*blocks[0], 0, columns, finish)
        sides_done(t - 1, 1)

        def rim(c):
            if t < STEPS:
                take_south(t - 1, c)
                rim_over(c, functools.partial(march, t))
                if t < STEPS - 1:
                    send_chunk(t, c)
                else:
                    send_last(c)
            else:
                pl.when(c > 0)(lambda: finish_rim(c - 1))
                pl.when(c == chunks - 1)(keep_last)
                take_south(t - 1, c)

                @pl.when(jnp.logical_or(c < chunks - 1, places["down"] < last_rank))
                def _():
                    rim_over(c, functools.partial(march, t))
                    send_rim_totals(c)

        each(chunks, rim)
        if t == STEPS - 1:
            each(lag, lambda c: south(t, 1 - first, chunks - lag + c).start())
        if t < STEPS:
            sides_start(t, (1, 2))
    keep_south()
    take_rim_totals(chunks - 1)
    keep_totals()
    done(u.at[:, pl.ds(0, 2), pl.ds(depth, cells), :], south_send)
    done(u.at[:, pl.ds(0, rows), pl.ds(0, both), :], side_send)
    upwards(lambda hop: done(totals, tot_send.at[hop - 1]))


def write_out(sizes, depth, pot, end, last_u, last_flows, last_halos, last_totals, pot_out, end_out,
              last_pot, last_end, sems):
    rows, cells, levels = pot.shape
    columns = cells // depth
    group = group_of(columns)
    width = chunk_of(columns, group)
    kept = cells - width * depth
    whole = ((pot, pot_out), (end, end_out))
    for i, (src, dst) in enumerate(whole):
        for y in range(1, rows - 1):
            pltpu.make_async_copy(src.at[y], dst.at[y], sems.at[i]).start()
        if kept:
            for y in (0, rows - 1):
                cut = (y, pl.ds(0, kept))
                pltpu.make_async_copy(src.at[cut], dst.at[cut], sems.at[i]).start()
    groups = width // group

    def last(i):
        side, x0 = i // groups, pl.multiple_of((i % groups) * group, group)
        values = new_values(depth, group, last_u, last_halos, *(last_flows.at[k] for k in (0, 1, 2)), 1, 3 * side, side, x0)
        for g, value in enumerate(values):
            own = pl.ds(pl.multiple_of((x0 + g) * depth, 8), depth)
            last_end[side, own, :] = value
            last_pot[side, own, :] = finished(sizes, last_totals, side, x0 + g, running_sum(value))

    each(2 * groups, last)
    for i, (src, (_, dst)) in enumerate(zip((last_pot, last_end), whole)):
        for side, y in ((0, 0), (1, rows - 1)):
            cut = (y, pl.ds(kept, cells - kept))
            pltpu.make_async_copy(src.at[side], dst.at[cut], sems.at[i]).start()
    for i, (src, dst) in enumerate(whole):
        pltpu.make_async_copy(src, dst, sems.at[i]).wait()


def local(sizes, field_values, *flows):
    rows, columns, depth, levels = field_values.shape
    cells = columns * depth
    width = chunk_of(columns, group_of(columns))
    flat = [array.reshape(rows, cells, levels) for array in (field_values, *flows)]
    block = pltpu.VMEM((rows, cells, levels), jnp.float32)
    dma = pltpu.SemaphoreType.DMA
    others = sizes["down"] - 1
    face = (rows, columns, levels)
    out = jax.ShapeDtypeStruct((rows, cells, levels), jnp.float32)
    in_vmem = pl.BlockSpec(memory_space=pltpu.VMEM)
    last = pltpu.VMEM((2, width * depth, levels), jnp.float32)
    held_shapes = (
        block, block,
        pltpu.VMEM((1, 6, (width + 2) * depth, levels), jnp.float32),
        pltpu.VMEM((3, 2, width * depth, levels), jnp.float32),
        pltpu.VMEM((1, 2, 2, width, levels), jnp.float32),
        pltpu.VMEM((others, 2, width, levels), jnp.float32),
    )
    held = pl.pallas_call(
        functools.partial(kernel, sizes, depth),
        out_shape=held_shapes,
        in_specs=[pl.BlockSpec(memory_space=pl.ANY)] * 4,
        out_specs=(in_vmem,) * len(held_shapes),
        scratch_shapes=[
            pltpu.VMEM((STEPS, rows + 2, cells + 2 * depth, levels), jnp.float32),
            block, block, block,
            pltpu.VMEM((STEPS, 2, *face), jnp.float32),
            pltpu.VMEM((STEPS, 2, *face), jnp.float32),
            pltpu.VMEM(face, jnp.float32),
            pltpu.VMEM((others, *face), jnp.float32),
            dma((4,)), dma((2, columns // width)), dma((2, 2)), dma((others, 1 + columns // width)),
            dma, dma, dma((others,)),
            pltpu.SemaphoreType.REGULAR,
        ],
        compiler_params=pltpu.CompilerParams(
            collective_id=0, has_side_effects=True, vmem_limit_bytes=48 * 1024 * 1024),
    )(*flat)
    results = pl.pallas_call(
        functools.partial(write_out, sizes, depth),
        out_shape=(out, out),
        in_specs=[in_vmem] * len(held_shapes),
        out_specs=(pl.BlockSpec(memory_space=pltpu.HBM),) * 2,
        scratch_shapes=[last, last, dma((2,))],
        compiler_params=pltpu.CompilerParams(vmem_limit_bytes=8 * 1024 * 1024),
    )(*held)
    return tuple(array.reshape(rows, columns, depth, levels) for array in results)


def solution(mesh):
    spec = P("south", "east", "down", None)
    sizes = {axis: mesh.shape[axis] for axis in AXES}
    return jax.shard_map(
        functools.partial(local, sizes), mesh=mesh, in_specs=(spec,) * 4,
        out_specs=(spec, spec), check_vma=False)
```

time: 74.6 us -> 74.2 us (level)
  no operation moved by 1% of the time
where the time goes in v2:
time: 74.2 us; the launch traced here: 74.1 us
  Pallas kernels  73.5 us (99%)
    pallas_call x1, Pallas kernels, local(): pl.pallas_call(functools.partial(kernel, sizes, depth), out_shape=held_sh...  70.8 us
    pallas_call x1, Pallas kernels, local(): pl.pallas_call(functools.partial(write_out, sizes, depth), out_shape=(out...  2.64 us

profile of v2, /device:TPU:5, one launch (start us, length us, event | category | flops | bytes accessed | tf_op | source)
XLA Modules:
  0.0 74.1 jit_solution(61994017003679315)
XLA Ops:
  0.6 70.8 %shard_map.59 = (f32[8,768,128]{2,1,0:T(8,128)S(1)}, f32[8,768,128]{2,1,0:T(8,128)S(1)}, f32[1,6,144,128]{3,2,1,0:T(8,128)S(1)}, f32[3,2,128,128]{3,2,1,0:T(8,12...) custom-call(f32[8,768,128]{2,1,0:T(8,128)} %bitcast.6, f32[8,768,128]{2,1,0:T(8,128)} %bitcast.7, ...), custom_call_target="tpu_custom_call" | custom-call | tf_op jit(solution)/shard_map/pallas_call | solution.py:446
  71.5 2.6 %shard_map.60 = (f32[8,768,128]{2,1,0:T(8,128)}, f32[8,768,128]{2,1,0:T(8,128)}) custom-call(f32[8,768,128]{2,1,0:T(8,128)S(1)} %get-tuple-element.10.pot, f32[8,768,128]{2,1,0:T(8,128)S(1)} %get-tuple-element.11.end, f32[1,6,144,128]{3,2,1,0:T(8,128)S(1)} %get-tuple-element.12.last_u, f32[3,2,128,128]{3,2,1,0:T(8,128)S(1)} %get-tuple-element.13.last_flows, ...), custom_call_target="tpu_custom_call" | custom-call | tf_op jit(solution)/shard_map/pallas_call | solution.py:465

commit v3 on v2

--- a/solution.py
+++ b/solution.py
@@ -101,12 +101,10 @@
 
         for axis, hop in hops:
             greet({**beside(axis, hop), "down": 0})
-        greeted = jnp.where(follows, 1, 2 * len(hops) + 1)
     else:
         hops += [("down", hop) for hop in range(1, sizes["down"])]
         for axis, hop in hops:
             greet(beside(axis, hop))
-        greeted = len(hops)
 
     def load(src, dst, sem):
         return pltpu.make_async_copy(src, dst, load_sem.at[sem])
@@ -114,28 +112,11 @@
     def done(ref, sem):
         pltpu.make_async_copy(ref, ref, sem).wait()
 
-    def rim_piece(side, start, count, sem):
-        y = (1 - side) * (rows - 1)
-        return load(field.at[y, pl.ds(start, count)], u.at[0, y + 1, pl.ds(depth + start, count), :], sem)
-
-    early = min(1, chunks)
-    head = early * width * depth
-    rest = [rim_piece(1 - near, 0, cells, 1)]
-    if head < cells:
-        rest.append(rim_piece(near, head, cells - head, 1))
-    inner = load(field.at[pl.ds(1, rows - 2)], u.at[0, pl.ds(2, rows - 2), pl.ds(depth, cells), :], 2)
-    flows = [load(src, dst, 3) for src, dst in ((flow_y, fy), (flow_x, fx), (flow_z, fz))]
-    rim_piece(near, 0, head, 0).start()
-    for copy in rest:
+    rims = [load(field.at[y], u.at[0, y + 1, pl.ds(depth, cells), :], 0) for y in (0, rows - 1)]
+    inner = load(field.at[pl.ds(1, rows - 2)], u.at[0, pl.ds(2, rows - 2), pl.ds(depth, cells), :], 1)
+    flows = [load(src, dst, 2) for src, dst in ((flow_y, fy), (flow_x, fx), (flow_z, fz))]
+    for copy in rims:
         copy.start()
-    done(u.at[0, 0, pl.ds(0, head), :], load_sem.at[0])
-    inner.start()
-    for copy in flows:
-        copy.start()
-    pl.semaphore_wait(barrier, greeted)
-
-    def rest_done():
-        done(u.at[pl.ds(0, 2), 0, pl.ds(0, cells - head // 2), :], load_sem.at[1])
 
     def chunk_at(c):
         return pl.ds(pl.multiple_of(c * width * depth + depth, 8), width * depth)
@@ -306,28 +287,35 @@
     if split:
         @pl.when(follows)
         def _():
-            each(early, lambda c: south(0, near, c).start())
-
+            pl.semaphore_wait(barrier, 1)
+            pltpu.make_async_remote_copy(
+                src_ref=field.at[(1 - near) * (rows - 1), pl.ds(0, width * depth), :],
+                dst_ref=u.at[0, near * (rows + 1), pl.ds(depth, width * depth), :],
+                send_sem=south_send, recv_sem=south_recv.at[0, 0], device_id=partner, device_id_type=MESH).start()
+    else:
+        pl.semaphore_wait(barrier, len(hops))
+    done(u.at[0, pl.ds(1, 2), pl.ds(depth, cells), :], load_sem.at[0])
+    inner.start()
+    for copy in flows:
+        copy.start()
+    if split:
         @pl.when(leads)
         def _():
+            pl.semaphore_wait(barrier, 2 * len(hops) + 1)
             pl.semaphore_signal(go, inc=1, device_id={"down": 1}, device_id_type=MESH)
-
-        rest_done()
 
         @pl.when(follows)
         def _():
-            each(chunks - early, lambda c: south(0, near, early + c).start())
-    else:
-        rest_done()
+            each(chunks - 1, lambda c: south(0, near, c + 1).start())
     pl.when(leads)(send_first)
-    done(u.at[0, pl.ds(2, rows - 2), pl.ds(depth, cells), :], load_sem.at[2])
+    done(u.at[0, pl.ds(2, rows - 2), pl.ds(depth, cells), :], load_sem.at[1])
     over(0, rows, 0, columns, functools.partial(take_faces, 0))
     if split:
         pl.when(follows)(lambda: pl.semaphore_wait(go, 1))
     sides_start(0, (0, 1, 2))
     if not split:
         pl.when(follows)(send_first)
-    done(u.at[pl.ds(0, 3), pl.ds(0, rows), pl.ds(depth, cells), :], load_sem.at[3])
+    done(u.at[pl.ds(0, 3), pl.ds(0, rows), pl.ds(depth, cells), :], load_sem.at[2])
 
     ahead = min(3, chunks) if split else 0
     if split:
@@ -455,7 +443,7 @@
             pltpu.VMEM((STEPS, 2, *face), jnp.float32),
             pltpu.VMEM(face, jnp.float32),
             pltpu.VMEM((others, *face), jnp.float32),
-            dma((4,)), dma((2, columns // width)), dma((2, 2)), dma((others, 1 + columns // width)),
+            dma((3,)), dma((2, columns // width)), dma((2, 2)), dma((others, 1 + columns // width)),
             dma, dma, dma((others,)),
             pltpu.SemaphoreType.REGULAR,
         ],

time: 74.2 us -> 73.9 us (level)
  no operation moved by 1% of the time
where the time goes in v3:
time: 73.9 us; the launch traced here: 73.7 us
  Pallas kernels  73 us (99%)
    pallas_call x1, Pallas kernels, local(): pl.pallas_call(functools.partial(kernel, sizes, depth), out_shape=held_sh...  70.4 us
    pallas_call x1, Pallas kernels, local(): pl.pallas_call(functools.partial(write_out, sizes, depth), out_shape=(out...  2.64 us

profile of v3, /device:TPU:5, one launch (start us, length us, event | category | flops | bytes accessed | tf_op | source)
XLA Modules:
  0.0 73.7 jit_solution(16858091078737004529)
XLA Ops:
  0.6 70.4 %shard_map.59 = (f32[8,768,128]{2,1,0:T(8,128)S(1)}, f32[8,768,128]{2,1,0:T(8,128)S(1)}, f32[1,6,144,128]{3,2,1,0:T(8,128)S(1)}, f32[3,2,128,128]{3,2,1,0:T(8,12...) custom-call(f32[8,768,128]{2,1,0:T(8,128)} %bitcast.6, f32[8,768,128]{2,1,0:T(8,128)} %bitcast.7, ...), custom_call_target="tpu_custom_call" | custom-call | tf_op jit(solution)/shard_map/pallas_call | solution.py:434
  71.0 2.6 %shard_map.60 = (f32[8,768,128]{2,1,0:T(8,128)}, f32[8,768,128]{2,1,0:T(8,128)}) custom-call(f32[8,768,128]{2,1,0:T(8,128)S(1)} %get-tuple-element.10.pot, f32[8,768,128]{2,1,0:T(8,128)S(1)} %get-tuple-element.11.end, f32[1,6,144,128]{3,2,1,0:T(8,128)S(1)} %get-tuple-element.12.last_u, f32[3,2,128,128]{3,2,1,0:T(8,128)S(1)} %get-tuple-element.13.last_flows, ...), custom_call_target="tpu_custom_call" | custom-call | tf_op jit(solution)/shard_map/pallas_call | solution.py:453

commit v4 on v3

--- a/solution.py
+++ b/solution.py
@@ -70,8 +70,8 @@
     return value * (1.0 / (value.shape[0] * sizes["down"]))
 
 
-def kernel(sizes, depth, field, flow_y, flow_x, flow_z, pot, end, last_u, last_flows, last_halos, last_totals,
-           u, fy, fx, fz, faces, halos, totals, totals_in, load_sem, south_recv, side_recv, tot_recv, south_send, side_send, tot_send, go):
+def kernel(sizes, depth, field, flow_y, flow_x, flow_z, pot, end, last_u, last_flows, last_halos, totals_in,
+           u, fy, fx, fz, faces, halos, totals, load_sem, south_recv, side_recv, tot_recv, south_send, side_send, tot_send, go):
     rows, cells, levels = field.shape
     columns = cells // depth
     group = group_of(columns)
@@ -242,17 +242,12 @@
     def send_rim_totals(c):
         def one(hop):
             for y in (0, rows - 1):
-                total(hop, 1 + c, y, 1, rim_at(c), width).start()
+                total(hop, 1, y, 1, rim_at(c), width).start()
 
         upwards(one)
 
-    def take_rim_totals(c):
-        from_below(lambda hop: done(totals_in.at[hop - 1, pl.ds(0, 2), pl.ds(rim_at(c), width)],
-                                    tot_recv.at[hop - 1, 1 + c]))
-
-    def finish_rim(c):
-        take_rim_totals(c)
-        rim_over(c, finish)
+    def take_rim_totals():
+        from_below(lambda hop: done(totals_in.at[hop - 1, pl.ds(0, 2)], tot_recv.at[hop - 1, 1]))
 
     base = columns - width
     last_cells = pl.ds(base * depth, width * depth)
@@ -273,19 +268,8 @@
             last_u[0, 5 * side, pl.ds(depth, width * depth), :] = u[
                 STEPS - 1, side * (rows + 1), pl.ds((base + 1) * depth, width * depth), :]
 
-    def keep_totals():
-        for hop in down_hops:
-            for side in (0, 1):
-                @pl.when(places["down"] >= hop)
-                def _():
-                    last_totals[hop - 1, side] = totals_in[hop - 1, side * (rows - 1), pl.ds(base, width), :]
-
-                @pl.when(places["down"] < hop)
-                def _():
-                    last_totals[hop - 1, side] = jnp.zeros((width, levels), jnp.float32)
-
     if split:
-        @pl.when(follows)
+        @pl.when(jnp.logical_and(follows, near == 1))
         def _():
             pl.semaphore_wait(barrier, 1)
             pltpu.make_async_remote_copy(
@@ -304,6 +288,11 @@
             pl.semaphore_wait(barrier, 2 * len(hops) + 1)
             pl.semaphore_signal(go, inc=1, device_id={"down": 1}, device_id_type=MESH)
 
+        @pl.when(jnp.logical_and(follows, near == 0))
+        def _():
+            pl.semaphore_wait(barrier, 1)
+            south(0, near, 0).start()
+
         @pl.when(follows)
         def _():
             each(chunks - 1, lambda c: south(0, near, c + 1).start())
@@ -318,11 +307,17 @@
     done(u.at[pl.ds(0, 3), pl.ds(0, rows), pl.ds(depth, cells), :], load_sem.at[2])
 
     ahead = min(3, chunks) if split else 0
-    if split:
+
+    def let_go():
         @pl.when(leads)
         def _():
             each(ahead, lambda c: south_done(0, c))
             pl.semaphore_signal(go, inc=1, device_id={"down": 1}, device_id_type=MESH)
+
+        @pl.when(follows)
+        def _():
+            pl.semaphore_wait(go, 1)
+            send_far()
 
     def take_south(t, c):
         if t == 0 and split:
@@ -332,13 +327,13 @@
 
     for t in range(1, STEPS + 1):
         sides_done(t - 1, 0)
-        over(*blocks[0], 0, columns, functools.partial(march, t))
         if t == 1 and split:
-            @pl.when(follows)
-            def _():
-                pl.semaphore_wait(go, 1)
-                send_far()
-
+            half = (rows - 2) // 2
+            over(1, half, 0, columns, functools.partial(march, t))
+            let_go()
+            over(1 + half, rows - 2 - half, 0, columns, functools.partial(march, t))
+        else:
+            over(*blocks[0], 0, columns, functools.partial(march, t))
         if t < STEPS:
             sides_start(t, (0,))
         else:
@@ -356,7 +351,6 @@
                 else:
                     send_last(c)
             else:
-                pl.when(c > 0)(lambda: finish_rim(c - 1))
                 pl.when(c == chunks - 1)(keep_last)
                 take_south(t - 1, c)
 
@@ -371,45 +365,57 @@
         if t < STEPS:
             sides_start(t, (1, 2))
     keep_south()
-    take_rim_totals(chunks - 1)
-    keep_totals()
+    take_rim_totals()
     done(u.at[:, pl.ds(0, 2), pl.ds(depth, cells), :], south_send)
     done(u.at[:, pl.ds(0, rows), pl.ds(0, both), :], side_send)
     upwards(lambda hop: done(totals, tot_send.at[hop - 1]))
 
 
-def write_out(sizes, depth, pot, end, last_u, last_flows, last_halos, last_totals, pot_out, end_out,
-              last_pot, last_end, sems):
+def write_out(sizes, depth, pot, end, last_u, last_flows, last_halos, totals_in, pot_out, end_out,
+              rim_pot, last_end, sems):
     rows, cells, levels = pot.shape
     columns = cells // depth
     group = group_of(columns)
     width = chunk_of(columns, group)
-    kept = cells - width * depth
-    whole = ((pot, pot_out), (end, end_out))
-    for i, (src, dst) in enumerate(whole):
+    base = columns - width
+    kept = base * depth
+    sides = ((0, 0), (1, rows - 1))
+
+    def write(i, src, dst):
+        pltpu.make_async_copy(src, dst, sems.at[i]).start()
+
+    for i, (src, dst) in enumerate(((pot, pot_out), (end, end_out))):
         for y in range(1, rows - 1):
-            pltpu.make_async_copy(src.at[y], dst.at[y], sems.at[i]).start()
-        if kept:
-            for y in (0, rows - 1):
-                cut = (y, pl.ds(0, kept))
-                pltpu.make_async_copy(src.at[cut], dst.at[cut], sems.at[i]).start()
-    groups = width // group
+            write(i, src.at[y], dst.at[y])
+    if kept:
+        for _, y in sides:
+            write(1, end.at[y, pl.ds(0, kept)], end_out.at[y, pl.ds(0, kept)])
+
+    def at(x):
+        return pl.ds(pl.multiple_of(x * depth, 8), depth)
 
     def last(i):
-        side, x0 = i // groups, pl.multiple_of((i % groups) * group, group)
-        values = new_values(depth, group, last_u, last_halos, *(last_flows.at[k] for k in (0, 1, 2)), 1, 3 * side, side, x0)
+        side, x0 = i % 2, pl.multiple_of((i // 2) * group, group)
+        flows = [last_flows.at[k] for k in (0, 1, 2)]
+        values = new_values(depth, group, last_u, last_halos, *flows, 1, 3 * side, side, x0)
         for g, value in enumerate(values):
-            own = pl.ds(pl.multiple_of((x0 + g) * depth, 8), depth)
-            last_end[side, own, :] = value
-            last_pot[side, own, :] = finished(sizes, last_totals, side, x0 + g, running_sum(value))
-
-    each(2 * groups, last)
-    for i, (src, (_, dst)) in enumerate(zip((last_pot, last_end), whole)):
-        for side, y in ((0, 0), (1, rows - 1)):
-            cut = (y, pl.ds(kept, cells - kept))
-            pltpu.make_async_copy(src.at[side], dst.at[cut], sems.at[i]).start()
-    for i, (src, dst) in enumerate(whole):
-        pltpu.make_async_copy(src, dst, sems.at[i]).wait()
+            last_end[side, at(x0 + g), :] = value
+            x = base + x0 + g
+            rim_pot[side, at(x), :] = finished(sizes, totals_in, side * (rows - 1), x, running_sum(value))
+
+    def before(i):
+        side, x0 = i % 2, pl.multiple_of((i // 2) * group, group)
+        y = side * (rows - 1)
+        for g in range(group):
+            rim_pot[side, at(x0 + g), :] = finished(sizes, totals_in, y, x0 + g, pot[y, at(x0 + g), :])
+
+    each(2 * (base // group), before)
+    each(2 * (width // group), last)
+    for side, y in sides:
+        write(0, rim_pot.at[side], pot_out.at[y])
+        write(1, last_end.at[side], end_out.at[y, pl.ds(kept, cells - kept)])
+    pltpu.make_async_copy(pot, pot_out, sems.at[0]).wait()
+    pltpu.make_async_copy(end, end_out, sems.at[1]).wait()
 
 
 def local(sizes, field_values, *flows):
@@ -429,7 +435,7 @@
         pltpu.VMEM((1, 6, (width + 2) * depth, levels), jnp.float32),
         pltpu.VMEM((3, 2, width * depth, levels), jnp.float32),
         pltpu.VMEM((1, 2, 2, width, levels), jnp.float32),
-        pltpu.VMEM((others, 2, width, levels), jnp.float32),
+        pltpu.VMEM((others, *face), jnp.float32),
     )
     held = pl.pallas_call(
         functools.partial(kernel, sizes, depth),
@@ -442,8 +448,7 @@
             pltpu.VMEM((STEPS, 2, *face), jnp.float32),
             pltpu.VMEM((STEPS, 2, *face), jnp.float32),
             pltpu.VMEM(face, jnp.float32),
-            pltpu.VMEM((others, *face), jnp.float32),
-            dma((3,)), dma((2, columns // width)), dma((2, 2)), dma((others, 1 + columns // width)),
+            dma((3,)), dma((2, columns // width)), dma((2, 2)), dma((others, 2)),
             dma, dma, dma((others,)),
             pltpu.SemaphoreType.REGULAR,
         ],
@@ -455,7 +460,7 @@
         out_shape=(out, out),
         in_specs=[in_vmem] * len(held_shapes),
         out_specs=(pl.BlockSpec(memory_space=pltpu.HBM),) * 2,
-        scratch_shapes=[last, last, dma((2,))],
+        scratch_shapes=[pltpu.VMEM((2, cells, levels), jnp.float32), last, dma((2,))],
         compiler_params=pltpu.CompilerParams(vmem_limit_bytes=8 * 1024 * 1024),
     )(*held)
     return tuple(array.reshape(rows, columns, depth, levels) for array in results)

time: 73.9 us -> 73.8 us (level)
  no operation moved by 1% of the time
where the time goes in v4:
time: 73.8 us; the launch traced here: 73.6 us
  Pallas kernels  73 us (99%)
    pallas_call x1, Pallas kernels, local(): pl.pallas_call(functools.partial(kernel, sizes, depth), out_shape=held_sh...  70.3 us
    pallas_call x1, Pallas kernels, local(): pl.pallas_call(functools.partial(write_out, sizes, depth), out_shape=(out...  2.64 us

profile of v4, /device:TPU:5, one launch (start us, length us, event | category | flops | bytes accessed | tf_op | source)
XLA Modules:
  0.0 73.6 jit_solution(3422122784761058360)
XLA Ops:
  0.6 70.3 %shard_map.59 = (f32[8,768,128]{2,1,0:T(8,128)S(1)}, f32[8,768,128]{2,1,0:T(8,128)S(1)}, f32[1,6,144,128]{3,2,1,0:T(8,128)S(1)}, f32[3,2,128,128]{3,2,1,0:T(8,12...) custom-call(f32[8,768,128]{2,1,0:T(8,128)} %bitcast.6, f32[8,768,128]{2,1,0:T(8,128)} %bitcast.7, ...), custom_call_target="tpu_custom_call" | custom-call | tf_op jit(solution)/shard_map/pallas_call | solution.py:440
  71.0 2.6 %shard_map.60 = (f32[8,768,128]{2,1,0:T(8,128)}, f32[8,768,128]{2,1,0:T(8,128)}) custom-call(f32[8,768,128]{2,1,0:T(8,128)S(1)} %get-tuple-element.10.pot, f32[8,768,128]{2,1,0:T(8,128)S(1)} %get-tuple-element.11.end, f32[1,6,144,128]{3,2,1,0:T(8,128)S(1)} %get-tuple-element.12.last_u, f32[3,2,128,128]{3,2,1,0:T(8,128)S(1)} %get-tuple-element.13.last_flows, ...), custom_call_target="tpu_custom_call" | custom-call | tf_op jit(solution)/shard_map/pallas_call | solution.py:458

commit v5 on v4

--- a/solution.py
+++ b/solution.py
@@ -71,7 +71,7 @@
 
 
 def kernel(sizes, depth, field, flow_y, flow_x, flow_z, pot, end, last_u, last_flows, last_halos, totals_in,
-           u, fy, fx, fz, faces, halos, totals, load_sem, south_recv, side_recv, tot_recv, south_send, side_send, tot_send, go):
+           u, fy, fx, fz, faces, halos, totals, south_recv, side_recv, tot_recv, south_send, side_send, tot_send, go):
     rows, cells, levels = field.shape
     columns = cells // depth
     group = group_of(columns)
@@ -107,14 +107,15 @@
             greet(beside(axis, hop))
 
     def load(src, dst, sem):
-        return pltpu.make_async_copy(src, dst, load_sem.at[sem])
+        return pltpu.make_async_copy(src, dst, sem)
 
     def done(ref, sem):
         pltpu.make_async_copy(ref, ref, sem).wait()
 
-    rims = [load(field.at[y], u.at[0, y + 1, pl.ds(depth, cells), :], 0) for y in (0, rows - 1)]
-    inner = load(field.at[pl.ds(1, rows - 2)], u.at[0, pl.ds(2, rows - 2), pl.ds(depth, cells), :], 1)
-    flows = [load(src, dst, 2) for src, dst in ((flow_y, fy), (flow_x, fx), (flow_z, fz))]
+    rims_sem, inner_sem, flows_sem = side_recv.at[1, 0], side_recv.at[1, 1], tot_recv.at[0, 0]
+    rims = [load(field.at[y], u.at[0, y + 1, pl.ds(depth, cells), :], rims_sem) for y in (0, rows - 1)]
+    inner = load(field.at[pl.ds(1, rows - 2)], u.at[0, pl.ds(2, rows - 2), pl.ds(depth, cells), :], inner_sem)
+    flows = [load(src, dst, flows_sem) for src, dst in ((flow_y, fy), (flow_x, fx), (flow_z, fz))]
     for copy in rims:
         copy.start()
 
@@ -278,7 +279,7 @@
                 send_sem=south_send, recv_sem=south_recv.at[0, 0], device_id=partner, device_id_type=MESH).start()
     else:
         pl.semaphore_wait(barrier, len(hops))
-    done(u.at[0, pl.ds(1, 2), pl.ds(depth, cells), :], load_sem.at[0])
+    done(u.at[0, pl.ds(1, 2), pl.ds(depth, cells), :], rims_sem)
     inner.start()
     for copy in flows:
         copy.start()
@@ -297,14 +298,14 @@
         def _():
             each(chunks - 1, lambda c: south(0, near, c + 1).start())
     pl.when(leads)(send_first)
-    done(u.at[0, pl.ds(2, rows - 2), pl.ds(depth, cells), :], load_sem.at[1])
+    done(u.at[0, pl.ds(2, rows - 2), pl.ds(depth, cells), :], inner_sem)
     over(0, rows, 0, columns, functools.partial(take_faces, 0))
     if split:
         pl.when(follows)(lambda: pl.semaphore_wait(go, 1))
     sides_start(0, (0, 1, 2))
     if not split:
         pl.when(follows)(send_first)
-    done(u.at[pl.ds(0, 3), pl.ds(0, rows), pl.ds(depth, cells), :], load_sem.at[2])
+    done(u.at[pl.ds(0, 3), pl.ds(0, rows), pl.ds(depth, cells), :], flows_sem)
 
     ahead = min(3, chunks) if split else 0
 
@@ -328,7 +329,7 @@
     for t in range(1, STEPS + 1):
         sides_done(t - 1, 0)
         if t == 1 and split:
-            half = (rows - 2) // 2
+            half = (rows - 2) // 6
             over(1, half, 0, columns, functools.partial(march, t))
             let_go()
             over(1 + half, rows - 2 - half, 0, columns, functools.partial(march, t))
@@ -448,7 +449,7 @@
             pltpu.VMEM((STEPS, 2, *face), jnp.float32),
             pltpu.VMEM((STEPS, 2, *face), jnp.float32),
             pltpu.VMEM(face, jnp.float32),
-            dma((3,)), dma((2, columns // width)), dma((2, 2)), dma((others, 2)),
+            dma((2, columns // width)), dma((2, 2)), dma((others, 2)),
             dma, dma, dma((others,)),
             pltpu.SemaphoreType.REGULAR,
         ],

time: 73.8 us -> 73.8 us (level)
  no operation moved by 1% of the time
where the time goes in v5:
time: 73.8 us; the launch traced here: 73.7 us
  Pallas kernels  73 us (99%)
    pallas_call x1, Pallas kernels, local(): pl.pallas_call(functools.partial(kernel, sizes, depth), out_shape=held_sh...  70.4 us
    pallas_call x1, Pallas kernels, local(): pl.pallas_call(functools.partial(write_out, sizes, depth), out_shape=(out...  2.64 us

profile of v5, /device:TPU:5, one launch (start us, length us, event | category | flops | bytes accessed | tf_op | source)
XLA Modules:
  0.0 73.7 jit_solution(14404877463858619632)
XLA Ops:
  0.6 70.4 %shard_map.59 = (f32[8,768,128]{2,1,0:T(8,128)S(1)}, f32[8,768,128]{2,1,0:T(8,128)S(1)}, f32[1,6,144,128]{3,2,1,0:T(8,128)S(1)}, f32[3,2,128,128]{3,2,1,0:T(8,12...) custom-call(f32[8,768,128]{2,1,0:T(8,128)} %bitcast.6, f32[8,768,128]{2,1,0:T(8,128)} %bitcast.7, ...), custom_call_target="tpu_custom_call" | custom-call | tf_op jit(solution)/shard_map/pallas_call | solution.py:441
  71.0 2.6 %shard_map.60 = (f32[8,768,128]{2,1,0:T(8,128)}, f32[8,768,128]{2,1,0:T(8,128)}) custom-call(f32[8,768,128]{2,1,0:T(8,128)S(1)} %get-tuple-element.10.pot, f32[8,768,128]{2,1,0:T(8,128)S(1)} %get-tuple-element.11.end, f32[1,6,144,128]{3,2,1,0:T(8,128)S(1)} %get-tuple-element.12.last_u, f32[3,2,128,128]{3,2,1,0:T(8,128)S(1)} %get-tuple-element.13.last_flows, ...), custom_call_target="tpu_custom_call" | custom-call | tf_op jit(solution)/shard_map/pallas_call | solution.py:459

commit v6 on v5

--- a/solution.py
+++ b/solution.py
@@ -17,7 +17,7 @@
 
 
 def chunk_of(columns, group):
-    return next(size for size in (2 * group, group) if columns % size == 0)
+    return next(size for size in (3 * group, 2 * group, group) if columns % size == 0)
 
 
 def each(count, body):
@@ -224,7 +224,7 @@
 
     last_block = sizes["south"] - 1
     first = jnp.where(places["south"] == last_block, 0, jnp.where(places["south"] == 1, 1, 1 - near))
-    lag = min(4, chunks)
+    lag = min(3, chunks)
 
     def send_chunk(t, c):
         south(t, 1 - near, c).start()
@@ -307,7 +307,7 @@
         pl.when(follows)(send_first)
     done(u.at[pl.ds(0, 3), pl.ds(0, rows), pl.ds(depth, cells), :], flows_sem)
 
-    ahead = min(3, chunks) if split else 0
+    ahead = min(2, chunks) if split else 0
 
     def let_go():
         @pl.when(leads)

time: 73.8 us -> 74 us (level)
  no operation moved by 1% of the time
where the time goes in v6:
time: 74 us; the launch traced here: 73.9 us
  Pallas kernels  73.2 us (99%)
    pallas_call x1, Pallas kernels, local(): pl.pallas_call(functools.partial(kernel, sizes, depth), out_shape=held_sh...  70.6 us
    pallas_call x1, Pallas kernels, local(): pl.pallas_call(functools.partial(write_out, sizes, depth), out_shape=(out...  2.64 us

profile of v6, /device:TPU:5, one launch (start us, length us, event | category | flops | bytes accessed | tf_op | source)
XLA Modules:
  0.0 73.9 jit_solution(71354893254718989)
XLA Ops:
  0.6 70.6 %shard_map.59 = (f32[8,768,128]{2,1,0:T(8,128)S(1)}, f32[8,768,128]{2,1,0:T(8,128)S(1)}, f32[1,6,208,128]{3,2,1,0:T(8,128)S(1)}, f32[3,2,192,128]{3,2,1,0:T(8,12...) custom-call(f32[8,768,128]{2,1,0:T(8,128)} %bitcast.6, f32[8,768,128]{2,1,0:T(8,128)} %bitcast.7, ...), custom_call_target="tpu_custom_call" | custom-call | tf_op jit(solution)/shard_map/pallas_call | solution.py:441
  71.2 2.6 %shard_map.60 = (f32[8,768,128]{2,1,0:T(8,128)}, f32[8,768,128]{2,1,0:T(8,128)}) custom-call(f32[8,768,128]{2,1,0:T(8,128)S(1)} %get-tuple-element.10.pot, f32[8,768,128]{2,1,0:T(8,128)S(1)} %get-tuple-element.11.end, f32[1,6,208,128]{3,2,1,0:T(8,128)S(1)} %get-tuple-element.12.last_u, f32[3,2,192,128]{3,2,1,0:T(8,128)S(1)} %get-tuple-element.13.last_flows, ...), custom_call_target="tpu_custom_call" | custom-call | tf_op jit(solution)/shard_map/pallas_call | solution.py:459
